TPU v7x, 256 devices: a whole 4x4x8 slice. The times are simulated.
256 devices in a mesh: grid: 64 (over z, x, core), band: 4 (over y).
Axes of the slice: x: 4, y: 4, z: 8, core: 2. Of those that a mesh axis runs over, the one named last changes fastest.
Arguments:
- basis: float32 [2048, 65536], P('band', 'grid'), as said below
- panel: float32 [1024, 65536], P('band', 'grid'), may hold values from -6 to 6
Outputs:
- new_panel: float32 [1024, 65536], P('band', 'grid')
- coeffs: float32 [2048, 1024], P('band')
Inputs may be any that keep to these rules, and one draw needn't show every extreme that they name: The rows of basis are orthogonal to each other, each with squared sum 65536 (to float32 rounding).
All inputs are finite; a program needn't handle non-finite values.
Results may differ from a plain program's by a relative error of at most 0.000073.
Values sent between devices are 32-bit elements; how exact they have to be, the bound alone decides.
No kernel may reach another device: no remote copies, remote signals or barrier semaphores. Data moves between devices by JAX's collectives and lax.ppermute only.
A program may use at most 128 MiB of HBM per device.

v0:
```python
import jax
import jax.numpy as jnp
from jax import lax
from jax.sharding import PartitionSpec as P


def together(arrays, axis):
    ravelled, at, finished = (jnp.concatenate([a.reshape(-1) for a in arrays]), 0, [])
    total = lax.psum(ravelled, axis)
    for a in arrays:
        finished.append(total[at : at + a.size].reshape(a.shape))
        at += a.size
    return tuple(finished)


def cut_along(array, dim, count):
    before, after = (array.shape[:dim], array.shape[dim + 1 :])
    return jnp.moveaxis(array.reshape(*before, count, -1, *after), dim, 0)


def summed_on_arrival(array, axis, dim):
    blocks = cut_along(array, dim, lax.axis_size(axis))
    arrived = lax.all_to_all(blocks, axis, split_axis=0, concat_axis=0, tiled=True)
    return arrived.sum(axis=0)


def tdot(left, right):
    return lax.dot_general(
        left,
        right,
        (((1,), (1,)), ((), ())),
        precision=lax.Precision.HIGHEST,
        preferred_element_type=jnp.float32,
    )


def ndot(left, right):
    return jnp.dot(left, right, precision=lax.Precision.HIGHEST)


def body(basis, panel):
    n_grid = panel.shape[1] * lax.axis_size("grid")
    n_band = lax.axis_size("band")
    rows_q = basis.shape[0]
    rows_p = panel.shape[0]
    n_panel = rows_p * n_band
    stacked = jnp.concatenate([basis, panel], 0)
    both = tdot(stacked, lax.all_gather(panel, "band", axis=0, tiled=True))
    coeff_sum, gram_sum = together((both[:rows_q], both[rows_q:]), "grid")
    coeffs = coeff_sum / n_grid
    projected = panel - lax.psum_scatter(
        ndot(coeffs.T, basis), "band", scatter_dimension=0, tiled=True
    )
    gram_part = gram_sum / n_grid - summed_on_arrival(ndot(coeffs.T, coeffs), "band", 0)
    gram = lax.all_gather(gram_part, "band", axis=0, tiled=True)
    factor = jnp.linalg.cholesky(gram)
    offset = lax.axis_index("band") * rows_p
    row_ids = lax.broadcasted_iota(jnp.int32, (n_panel, rows_p), 0)
    col_ids = lax.broadcasted_iota(jnp.int32, (n_panel, rows_p), 1)
    unit_cols = (row_ids == col_ids + offset).astype(jnp.float32)
    inverse_rows = lax.linalg.triangular_solve(
        factor, unit_cols, left_side=True, lower=True, transpose_a=True
    ).T
    new_panel = ndot(inverse_rows, lax.all_gather(projected, "band", axis=0, tiled=True))
    return (new_panel, coeffs)


def solution(mesh):
    placed = (P("band", "grid"), P("band", "grid"))
    return jax.shard_map(
        body,
        mesh=mesh,
        in_specs=placed,
        out_specs=(P("band", "grid"), P("band", None)),
        check_vma=False,
    )
```

profile of v0, /device:TPU:57, one launch (start us, length us, event | category | flops | bytes accessed | tf_op | source)
XLA Modules:
  0.0 781.4 jit_solution(712397003574629770)
XLA Ops:
  7.9 53.2 %all-gather.4.cloned.1.call-done = f32[1024,1024]{1,0:T(8,128)} async-done(((f32[256,1024]{1,0:T(8,128)}), f32[1024,1024]{1,0:T(8,128)}) %all-gather.4.cloned.1.call-update) | async-done | bytes 4194320 | tf_op jit(solution)/shard_map/all_gather | solution.py:48
  61.1 12.5 %fusion.1 = f32[768,1024]{1,0:T(8,128)S(1)} fusion(f32[1024,1024]{1,0:T(8,128)} %all-gather.4.cloned.1.call-done, f32[256,1024]{1,0:T(8,128)} %param.3, f32[512,1024]{1,0:T(8,128)} %param.2), kind=kOutput, calls=%fused_computation.6 | convolution fusion | flops 9664462848 | bytes 10485760 | tf_op jit(solution)/shard_map/dot_general | solution.py:28
  76.9 193.9 %all-reduce.3.cloned.1.call-done = f32[786432]{0:T(1024)} async-done(((f32[786432]{0:T(1024)}), f32[786432]{0:T(1024)}) %all-reduce.3.cloned.1.call-update) | async-done | bytes 3145744 | tf_op jit(solution)/shard_map/psum | solution.py:9
  274.1 10.2 %fusion.69 = f32[1024,1024]{1,0:T(8,128)} fusion(f32[512,1024]{1,0:T(8,128)} %div.29, f32[512,1024]{1,0:T(8,128)} %param.2), kind=kOutput, calls=%fused_computation.169 | convolution fusion | flops 6442450944 | bytes 8388608 | tf_op jit(solution)/shard_map/dot_general | solution.py:38
  285.8 3.1 copy.13
  288.9 9.9 %fusion.68 = f32[4,256,1024]{2,1,0:T(8,128)} fusion(f32[4,256,512]{2,1,0:T(8,128)} %bitcast.110, f32[512,1024,1]{1,0,2:T(8,128)S(1)} %copy-done.2), kind=kOutput, calls=%fused_computation.168 | convolution fusion | flops 6442450944 | bytes 8388608 | tf_op jit(solution)/shard_map/dot_general | solution.py:38
  298.7 5.1 all-to-all-start
  305.7 70.9 %all-to-all-done = f32[4,256,1024]{2,1,0:T(8,128)} async-done(((f32[4,256,1024]{2,1,0:T(8,128)}), f32[4,256,1024]{2,1,0:T(8,128)}, u32[]{:S(2)}, u32[]{:S(2)}) %all-to-all-start) | async-done | bytes 4194336 | tf_op jit(solution)/shard_map/all_to_all | solution.py:23
  376.6 3.7 reduce_sum.9
  383.4 2.4 sub.7
  385.9 47.1 %all-gather.6.cloned.1.call-done = f32[1024,1024]{0,1:T(8,128)} async-done(((f32[256,1024]{0,1:T(8,128)}), f32[1024,1024]{0,1:T(8,128)}) %all-gather.6.cloned.1.call-update) | async-done | bytes 4194320 | tf_op jit(solution)/shard_map/all_gather | solution.py:55
  433.0 5.5 copy.12
  438.5 4.4 fusion
  444.9 11.7 %cholesky.223 = f32[128,128]{1,0:T(8,128)S(1)} custom-call(f32[128,128]{1,0:T(8,128)S(1)} %cholesky.580), custom_call_target="Cholesky" | custom-call | tf_op jit(solution)/shard_map/jit(cholesky)/cholesky | solution.py:56
  456.6 2.5 cholesky.255
  459.1 9.8 %custom-call.62 = f32[1,128,128]{1,2,0:T(8,128)S(1)} custom-call(f32[1,128,128]{2,1,0:T(8,128)S(1)} %get-tuple-element.41), custom_call_target="InvertDiagBlocksLowerTriangular" | custom-call | tf_op jit(solution)/shard_map/jit(cholesky)/cholesky | solution.py:56
  469.0 2.3 constant_dynamic-update-slice_fusion.32
  472.9 11.9 %cholesky.244 = f32[128,128]{1,0:T(8,128)S(1)} custom-call(f32[128,128]{1,0:T(8,128)S(1)} %cholesky.584), custom_call_target="Cholesky" | custom-call | tf_op jit(solution)/shard_map/jit(cholesky)/cholesky | solution.py:56
  485.4 9.8 %custom-call.63 = f32[1,128,128]{1,2,0:T(8,128)S(1)} custom-call(f32[1,128,128]{2,1,0:T(8,128)S(1)} %get-tuple-element.38), custom_call_target="InvertDiagBlocksLowerTriangular" | custom-call | tf_op jit(solution)/shard_map/jit(cholesky)/cholesky | solution.py:56
  496.5 2.1 convolution_subtract_fusion.1
  498.6 11.7 %cholesky.468 = f32[128,128]{1,0:T(8,128)S(1)} custom-call(f32[128,128]{1,0:T(8,128)S(1)} %cholesky.589), custom_call_target="Cholesky" | custom-call | tf_op jit(solution)/shard_map/jit(cholesky)/cholesky | solution.py:56
  511.6 9.8 %custom-call.64 = f32[1,128,128]{1,2,0:T(8,128)S(1)} custom-call(f32[1,128,128]{2,1,0:T(8,128)S(1)} %get-tuple-element.35), custom_call_target="InvertDiagBlocksLowerTriangular" | custom-call | tf_op jit(solution)/shard_map/jit(cholesky)/cholesky | solution.py:56
  522.6 2.3 convolution_subtract_fusion.2
  524.9 12.1 %cholesky.487 = f32[128,128]{1,0:T(8,128)S(1)} custom-call(f32[128,128]{1,0:T(8,128)S(1)} %cholesky.594), custom_call_target="Cholesky" | custom-call | tf_op jit(solution)/shard_map/jit(cholesky)/cholesky | solution.py:56
  538.3 9.8 %custom-call.65 = f32[1,128,128]{1,2,0:T(8,128)S(1)} custom-call(f32[1,128,128]{2,1,0:T(8,128)S(1)} %get-tuple-element.32), custom_call_target="InvertDiagBlocksLowerTriangular" | custom-call | tf_op jit(solution)/shard_map/jit(cholesky)/cholesky | solution.py:56
  549.2 2.4 convolution_subtract_fusion.3
  551.6 11.7 %cholesky.506 = f32[128,128]{1,0:T(8,128)S(1)} custom-call(f32[128,128]{1,0:T(8,128)S(1)} %cholesky.599), custom_call_target="Cholesky" | custom-call | tf_op jit(solution)/shard_map/jit(cholesky)/cholesky | solution.py:56
  564.6 9.9 %custom-call.66 = f32[1,128,128]{1,2,0:T(8,128)S(1)} custom-call(f32[1,128,128]{2,1,0:T(8,128)S(1)} %get-tuple-element.29), custom_call_target="InvertDiagBlocksLowerTriangular" | custom-call | tf_op jit(solution)/shard_map/jit(cholesky)/cholesky | solution.py:56
  575.6 2.3 convolution_subtract_fusion.4
  577.9 11.7 %cholesky.526 = f32[128,128]{1,0:T(8,128)S(1)} custom-call(f32[128,128]{1,0:T(8,128)S(1)} %cholesky.604), custom_call_target="Cholesky" | custom-call | tf_op jit(solution)/shard_map/jit(cholesky)/cholesky | solution.py:56
  590.8 9.8 %custom-call.67 = f32[1,128,128]{1,2,0:T(8,128)S(1)} custom-call(f32[1,128,128]{2,1,0:T(8,128)S(1)} %get-tuple-element.26), custom_call_target="InvertDiagBlocksLowerTriangular" | custom-call | tf_op jit(solution)/shard_map/jit(cholesky)/cholesky | solution.py:56
  601.6 2.0 convolution_subtract_fusion.11
  603.6 11.9 %cholesky.546 = f32[128,128]{1,0:T(8,128)S(1)} custom-call(f32[128,128]{1,0:T(8,128)S(1)} %cholesky.609), custom_call_target="Cholesky" | custom-call | tf_op jit(solution)/shard_map/jit(cholesky)/cholesky | solution.py:56
  616.9 9.8 %custom-call.68 = f32[1,128,128]{1,2,0:T(8,128)S(1)} custom-call(f32[1,128,128]{2,1,0:T(8,128)S(1)} %get-tuple-element.23), custom_call_target="InvertDiagBlocksLowerTriangular" | custom-call | tf_op jit(solution)/shard_map/jit(cholesky)/cholesky | solution.py:56
  629.3 11.7 %cholesky.564 = f32[128,128]{1,0:T(8,128)S(1)} custom-call(f32[128,128]{1,0:T(8,128)S(1)} %convolution_subtract_fusion.13), custom_call_target="Cholesky" | custom-call | tf_op jit(solution)/shard_map/jit(cholesky)/cholesky | solution.py:56
  647.9 4.8 select_select_fusion
  652.7 22.6 %while.1 = (s32[]{:T(128)}, f32[1024,1024]{1,0:T(8,128)}, s32[8,2]{0,1:T(2,128)S(1)}, f32[8,128,128]{2,1,0:T(8,128)S(1)}, s32[]{:T(128)}) while((s32[]{:T(128)}, f32[1024,1024]{1,0:T(8,128)}, s32[8,2]{0,1:T(2,128)S(1)}, f32[8,128,128]{2,1,0:T(8,128)S(1)}, s32[]{:T(128)}) %tuple.43), condition=%wide.while_cond, body=%wide.while_body.sunk | while | flops 2 | bytes 131181 | solution.py:61
  653.3 2.2 bitcast_dynamic-update-slice_fusion.2
  656.1 2.2 bitcast_dynamic-update-slice_fusion.2
  659.0 2.2 bitcast_dynamic-update-slice_fusion.2
  661.8 2.2 bitcast_dynamic-update-slice_fusion.2
  664.6 2.2 bitcast_dynamic-update-slice_fusion.2
  667.5 2.2 bitcast_dynamic-update-slice_fusion.2
  670.3 2.2 bitcast_dynamic-update-slice_fusion.2
  673.1 2.1 bitcast_dynamic-update-slice_fusion.2
  675.3 78.8 %custom-call.69 = f32[8,128,128]{1,2,0:T(8,128)S(1)} custom-call(f32[8,128,128]{2,1,0:T(8,128)S(1)} %get-tuple-element.9), custom_call_target="InvertDiagBlocksLowerTriangular" | custom-call | tf_op jit(solution)/shard_map/triangular_solve | solution.py:61
  765.3 2.0 convolution_subtract_fusion.12
  767.7 6.8 fusion.70
  (118 shorter events, 50.4 us)
Async XLA Ops:
  7.2 54.0 %all-gather.4.cloned.1.call-start = ((), (), s32[]{:S(2)}) async-start(), calls=%async_computation.2 | async-start | bytes 5242880 | tf_op jit(solution)/shard_map/all_gather | solution.py:48
  7.9 262.9 %all-reduce.3.cloned.1.call-start = ((), (), s32[]{:S(2)}) async-start(), calls=%async_computation.3 | async-start | bytes 6291456 | tf_op jit(solution)/shard_map/psum | solution.py:9
  76.4 307.0 %reduce-scatter.2.cloned.1.call-start = ((), (), s32[]{:S(2)}) async-start(), calls=%async_computation.5 | async-start | bytes 5242880 | tf_op jit(solution)/shard_map/reduce_scatter | solution.py:51
  285.8 3.1 copy-start.2
  298.7 77.9 %all-to-all-start = ((f32[4,256,1024]{2,1,0:T(8,128)}), f32[4,256,1024]{2,1,0:T(8,128)}, u32[]{:S(2)}, u32[]{:S(2)}) async-start(f32[4,256,1024]{2,1,0:T(8,128)} %fusion.68), calls=%async_computation | async-start | bytes 8388608 | tf_op jit(solution)/shard_map/all_to_all | solution.py:23
  303.9 129.1 %all-gather.6.cloned.1.call-start = ((), (), s32[]{:S(2)}) async-start(), calls=%async_computation.4 | async-start | bytes 5242880 | tf_op jit(solution)/shard_map/all_gather | solution.py:55
  380.3 3.1 copy-start.1
  383.1 384.6 %all-gather.8.cloned.1.call-start = ((), (), s32[]{:S(2)}) async-start(), calls=%async_computation.6 | async-start | bytes 5242880 | tf_op jit(solution)/shard_map/all_gather | solution.py:64
  442.9 2.0 copy-start
Sparse Core Ops, SparseCore 0:
  9.8 51.2 all-gather.3
  76.6 194.2 all-reduce.2
  284.4 72.3 reduce-scatter.1
  383.2 49.7 all-gather.5
  434.6 51.4 all-gather.7
where the time goes:
time: 791 us; the launch traced here: 781 us
  waiting for transfers between devices  366 us (46%)
  other arithmetic  273 us (35%)
  matrix products  75.5 us (10%)
  local copies, waits for them, and re-layouts  41.8 us (5%)
  between operations  19.7 us (2%)
    psum x1, waiting for transfers between devices, together(): total = lax.psum(ravelled, axis)  194 us
    another operation x30, other arithmetic, body(): factor = jnp.linalg.cholesky(gram)  172 us
    another operation x3, other arithmetic, body(): lax.linalg.triangular_solve(factor, unit_cols, left_side=True, lower=True...  83.7 us
    all_to_all x1, waiting for transfers between devices, summed_on_arrival(): lax.all_to_all(blocks, axis, split_axis=0, concat_axis=0, tiled=True)  70.9 us
    all_gather x1, waiting for transfers between devices, body(): both = tdot(stacked, lax.all_gather(panel, 'band', axis=0, tiled=True))  53.2 us
    all_gather x1, waiting for transfers between devices, body(): gram = lax.all_gather(gram_part, 'band', axis=0, tiled=True)  47.1 us
    dot_general x3, matrix products, ndot(): return jnp.dot(left, right, precision=lax.Precision.HIGHEST)  26.8 us
    another operation x14, matrix products, body(): factor = jnp.linalg.cholesky(gram)  23.1 us
  transfers between devices with their start and end apart: 6, of which 4 were waited for; matrix products, arithmetic and copies ran while one was open for 45% of the time, Pallas kernels for 0%

commit v1 on v0

v1 whole, which is shorter than its diff:
```python
import jax
import jax.numpy as jnp
from jax import lax
from jax.experimental import pallas as pl
from jax.experimental.pallas import tpu as pltpu
from jax.sharding import Mesh, PartitionSpec as P

Z, X, C, B = 8, 4, 2, 4
GRID = ("z", "x", "c")
BLK = 128
HI = lax.Precision.HIGHEST
F32 = jnp.float32
VMEM = pl.BlockSpec(memory_space=pltpu.VMEM)
SMEM = pl.BlockSpec(memory_space=pltpu.SMEM)


def params(mib):
    return pltpu.CompilerParams(vmem_limit_bytes=mib * 1024 * 1024)


def shift(array, axis, count, by):
    return lax.ppermute(array, axis, [(i, (i + by) % count) for i in range(count)])


def tdot(left, right):
    return lax.dot_general(left, right, (((1,), (1,)), ((), ())), precision=HI, preferred_element_type=F32)


def cdot(left, right):
    return lax.dot_general(left, right, (((0,), (0,)), ((), ())), precision=HI, preferred_element_type=F32)


def rotate_body(ids_ref, basis_ref, panel_ref, out_ref):
    c, x, z = ids_ref[1], ids_ref[2], ids_ref[3]

    def place(t):
        return lax.rem(x + lax.rem(t // Z, X), X) * Z + lax.rem(z + lax.rem(t, Z), Z)

    def from_basis(t, carry):
        out_ref[t] = basis_ref[lax.rem(c + t // (X * Z), C) * (X * Z) + place(t)]
        return carry

    def from_panel(t, carry):
        out_ref[C * X * Z + t] = panel_ref[place(t)]
        return carry

    lax.fori_loop(0, C * X * Z, from_basis, 0)
    lax.fori_loop(0, X * Z, from_panel, 0)


def rotate(ids, basis, panel):
    nq, pts = basis.shape
    np_, _ = panel.shape
    out = pl.pallas_call(
        rotate_body,
        out_shape=jax.ShapeDtypeStruct(((nq + np_) // 8, 8, pts), F32),
        in_specs=[SMEM, VMEM, VMEM],
        out_specs=VMEM,
        compiler_params=params(16),
        name="rotate",
    )(ids, basis.reshape(nq // 8, 8, pts), panel.reshape(np_ // 8, 8, pts))
    return out.reshape(nq + np_, pts)


def unrotate_body(ids_ref, near_ref, far_ref, out_ref):
    b, c, x, z = ids_ref[0], ids_ref[1], ids_ref[2], ids_ref[3]
    width = out_ref.shape[2] // B
    for dc, ref in ((0, near_ref), (1, far_ref)):

        def one(t, carry):
            xx = lax.rem(x + t // Z, X)
            zz = lax.rem(z + lax.rem(t, Z), Z)
            dst = (lax.rem(c + dc, C) * X + xx) * Z + zz
            for s in range(B):
                at = pl.multiple_of(lax.rem(b + s, B) * width, width)
                out_ref[dst, :, pl.ds(at, width)] = ref[t, :, s * width : (s + 1) * width]
            return carry

        lax.fori_loop(0, X * Z, one, 0)


def unrotate(ids, near, far):
    rows, cols = near.shape
    out = pl.pallas_call(
        unrotate_body,
        out_shape=jax.ShapeDtypeStruct((2 * rows // 8, 8, cols), F32),
        in_specs=[SMEM, VMEM, VMEM],
        out_specs=VMEM,
        compiler_params=params(16),
        name="unrotate",
    )(ids, near.reshape(rows // 8, 8, cols), far.reshape(rows // 8, 8, cols))
    return out.reshape(2 * rows, cols)


def squares_body(ids_ref, near_ref, far_ref, out_ref, acc_ref):
    c, x, z = ids_ref[1], ids_ref[2], ids_ref[3]
    width = near_ref.shape[1] // B
    row = x * (8 * Z) + z * 8
    block = row // BLK
    inner = pl.multiple_of(row - block * BLK, 8)
    for s in range(B):
        at = pl.multiple_of(s * width + block * BLK, BLK)
        acc_ref[...] = cdot(near_ref[:, pl.ds(at, BLK)], near_ref[...]) + cdot(far_ref[:, pl.ds(at, BLK)], far_ref[...])
        for h in range(2):
            a = (s + h) % B
            d = (s + 2 + h) % B
            low = acc_ref[pl.ds(inner, 8), a * width : (a + 1) * width]
            high = acc_ref[pl.ds(inner, 8), d * width : (d + 1) * width]
            out_ref[s, :, h * width : (h + 1) * width] = jnp.where(c == 0, low, high)


def squares(ids, near, far):
    cols = near.shape[1]
    return pl.pallas_call(
        squares_body,
        out_shape=jax.ShapeDtypeStruct((B, 8, cols // 2), F32),
        in_specs=[SMEM, VMEM, VMEM],
        out_specs=VMEM,
        scratch_shapes=[pltpu.VMEM((BLK, cols), F32)],
        compiler_params=params(24),
        name="squares",
    )(ids, near, far)


def project_body(ids_ref, near_ref, far_ref, basis_ref, panel_ref, out_ref):
    half = near_ref.shape[0]
    out_ref[...] = cdot(near_ref[...], basis_ref[:half]) + cdot(far_ref[...], basis_ref[half:])

    @pl.when(pl.program_id(0) == 0)
    def _():
        out_ref[...] = out_ref[...] - panel_ref[...]


def project(ids, near, far, stacked, panel):
    half, cols = near.shape
    rows, pts = panel.shape
    return pl.pallas_call(
        project_body,
        out_shape=jax.ShapeDtypeStruct((cols, pts), F32),
        grid_spec=pltpu.PrefetchScalarGridSpec(
            num_scalar_prefetch=1,
            grid=(B,),
            in_specs=[
                pl.BlockSpec((half, rows), lambda s, ids: (0, s)),
                pl.BlockSpec((half, rows), lambda s, ids: (0, s)),
                pl.BlockSpec((2 * half, pts), lambda s, ids: (0, 0)),
                pl.BlockSpec((rows, pts), lambda s, ids: (0, 0)),
            ],
            out_specs=pl.BlockSpec((rows, pts), lambda s, ids: (lax.rem(ids[0] + s, B), 0)),
        ),
        compiler_params=params(32),
        name="project",
    )(ids, near, far, stacked, panel)


def lane_splat(tile, c):
    return jnp.broadcast_to(tile[:, c : c + 1], tile.shape)


def row_splat(tile, k):
    return jnp.broadcast_to(tile[k : k + 1, :], tile.shape)


def unit_inverse(tiles):
    n = len(tiles)
    tiles = list(tiles)
    sub = lax.broadcasted_iota(jnp.int32, (8, BLK), 0)
    lane = lax.broadcasted_iota(jnp.int32, (8, BLK), 1)
    zero = jnp.zeros((8, BLK), F32)
    one = jnp.ones((8, BLK), F32)
    scale = [None] * n
    for jb in range(n):
        j0 = 8 * jb
        inside = (lane >= j0) & (lane < j0 + 8)
        cols = {r: [lane_splat(tiles[r], j0 + k) for k in range(8)] for r in range(jb, n)}
        panel = jnp.where(inside, jnp.where(lane - j0 == sub, one, zero), tiles[jb])
        mult = {r: [None] * 8 for r in range(jb, n)}
        rows = []
        diag = zero
        for k in range(8):
            pivot = row_splat(cols[jb][k], k)
            recip = 1.0 / pivot
            diag = jnp.where(sub == k, pivot, diag)
            row = row_splat(panel, k)
            rows.append(row)
            for r in range(jb, n):
                m = cols[r][k] * recip
                mult[r][k] = jnp.where(sub > k, m, zero) if r == jb else m
            if k < 7:
                panel = panel - mult[jb][k] * row
            for q in range(k + 1, 8):
                f = row_splat(cols[jb][q], k)
                for r in range(jb, n):
                    cols[r][q] = cols[r][q] - mult[r][k] * f
        for r in range(jb + 1, n):
            a = jnp.where(inside, zero, tiles[r])
            for k in range(8):
                a = a - mult[r][k] * rows[k]
            tiles[r] = a
        tiles[jb] = panel
        scale[jb] = lax.rsqrt(diag)
    return [jnp.where(lane <= 8 * r + sub, tiles[r], zero) * scale[r] for r in range(n)]


def factor_body(ids_ref, near_ref, far_ref, out_ref, m_ref, r_ref):
    b, c, x, z = ids_ref[0], ids_ref[1], ids_ref[2], ids_ref[3]
    nb = m_ref.shape[0]
    per_band = nb // B
    for dc, ref in ((0, near_ref), (1, far_ref)):
        cc = lax.rem(c + dc, C)

        def take(t, carry):
            xx = lax.rem(x + t // Z, X)
            zz = lax.rem(z + lax.rem(t, Z), Z)
            for db in range(B):
                bb = lax.rem(b + db, B)
                row = pl.multiple_of(bb * (per_band * BLK) + (xx * Z + zz) * 8, 8)
                for m in range(nb // 2):
                    col = lax.rem(bb + 2 * cc + m // per_band, B) * per_band + m % per_band
                    m_ref[col, pl.ds(row, 8), :] = ref[t * B + db, :, m * BLK : (m + 1) * BLK]
            return carry

        lax.fori_loop(0, X * Z, take, 0)

    def step(k, carry):
        base = pl.multiple_of(k * BLK, BLK)
        tiles = [m_ref[k, pl.ds(base + 8 * r, 8), :] for r in range(BLK // 8)]
        inv = jnp.concatenate(unit_inverse(tiles), 0)
        line = jnp.concatenate([m_ref[cb, pl.ds(base, BLK), :] for cb in range(nb)], 1)
        prod = jnp.dot(inv, line, precision=HI, preferred_element_type=F32)
        for cb in range(nb):
            r_ref[cb] = jnp.where(cb == k, inv, prod[:, cb * BLK : (cb + 1) * BLK])

        @pl.when(k // per_band == b)
        def _():
            at = pl.multiple_of(lax.rem(k, per_band) * BLK, BLK)
            for cb in range(nb):
                out_ref[pl.ds(at, BLK), cb * BLK : (cb + 1) * BLK] = jnp.where(cb <= k, -r_ref[cb], 0.0)

        m_ref[k] = jnp.zeros(m_ref.shape[1:], F32)

        def trail(i, carry):
            ib = pl.multiple_of(i * BLK, BLK)
            full = jnp.concatenate([r_ref[cb] for cb in range(nb)], 1)
            update = cdot(r_ref[i], full)
            for cb in range(nb):
                m_ref[cb, pl.ds(ib, BLK), :] = m_ref[cb, pl.ds(ib, BLK), :] - update[:, cb * BLK : (cb + 1) * BLK]
            return carry

        lax.fori_loop(k + 1, nb, trail, 0)
        return carry

    lax.fori_loop(0, nb, step, 0)


def factor_rows(ids, near, far, n):
    return pl.pallas_call(
        factor_body,
        out_shape=jax.ShapeDtypeStruct((n // B, n), F32),
        in_specs=[SMEM, VMEM, VMEM],
        out_specs=VMEM,
        scratch_shapes=[pltpu.VMEM((n // BLK, n, BLK), F32), pltpu.VMEM((n // BLK, BLK, BLK), F32)],
        compiler_params=params(40),
        name="factor_rows",
    )(ids, near, far)


def spread(count):
    return [(s, s if 2 * s <= count else s - count) for s in range(1, count)]


def ring4(piece, axis):
    half = piece.shape[0] // 2
    after = shift(piece, axis, 4, -1)
    before = shift(piece, axis, 4, 1)
    low = shift(after[:half], axis, 4, -1)
    high = shift(before[half:], axis, 4, 1)
    return [piece, after, jnp.concatenate([low, high], 0), before]


def gather_z(piece):
    return [piece] + [shift(piece, "z", Z, -by) for _, by in spread(Z)]


def body(basis, panel):
    rows_p, pts = panel.shape
    n_panel = rows_p * B
    n_grid = pts * Z * X * C
    core = lax.axis_index("c")
    ids = jnp.stack([lax.axis_index(a) for a in ("b", "c", "x", "z")]).astype(jnp.int32)
    chunks = ring4(panel, "b")
    stacked = rotate(ids, basis, panel)
    rows_q = basis.shape[0]
    half_q = rows_q // 2
    parts = [tdot(stacked, chunk) for chunk in chunks]
    grams = [part[rows_q:] for part in parts]
    first = core == 0
    keep = [part[:half_q] for part in parts] + [jnp.where(first, grams[i], grams[i + 2]) for i in range(2)]
    give = [part[half_q:rows_q] for part in parts] + [jnp.where(first, grams[i + 2], grams[i]) for i in range(2)]
    mine = jnp.concatenate(keep, 1) + shift(jnp.concatenate(give, 1), "c", C, 1)
    wide = mine.shape[1]
    mine = mine.reshape(X, -1, wide)
    mid = mine.shape[1] // 2
    far2 = jnp.concatenate([shift(mine[2, :mid], "x", X, 2), shift(mine[2, mid:], "x", X, -2)], 0)
    mine = mine[0] + shift(mine[1], "x", X, 1) + shift(mine[3], "x", X, -1) + far2
    mine = mine.reshape(Z, -1, wide)
    total = mine[0]
    for s, by in spread(Z):
        total = total + shift(mine[s], "z", Z, by)
    total = total / n_grid
    own = total[:, :n_panel]
    own_gram = total[:, n_panel:]

    own = jnp.concatenate(gather_z(own), 0)
    near = jnp.concatenate(ring4(own, "x"), 0)
    far = shift(near, "c", C, 1)

    pieces = squares(ids, near, far)
    own_gram = own_gram - pieces[0]
    for s, by in spread(B):
        own_gram = own_gram - shift(pieces[s], "b", B, by)
    own_gram = jnp.concatenate([own_gram] + [shift(own_gram, "b", B, -by) for _, by in spread(B)], 0)
    own_gram = jnp.concatenate(gather_z(own_gram), 0)
    near_gram = jnp.concatenate(ring4(own_gram, "x"), 0)
    far_gram = shift(near_gram, "c", C, 1)

    short = lax.psum(project(ids, near, far, stacked[:rows_q], panel), "b")
    coeffs = unrotate(ids, near, far)
    tiled = (-1, 8, near_gram.shape[1])
    rows = factor_rows(ids, near_gram.reshape(tiled), far_gram.reshape(tiled), n_panel)
    new_panel = jnp.dot(rows, short, precision=HI, preferred_element_type=F32)
    return (new_panel, coeffs)


def solution(mesh):
    fine = Mesh(mesh.devices.reshape(Z, X, C, B), GRID + ("b",))
    placed = (P("b", GRID), P("b", GRID))
    return jax.shard_map(
        body,
        mesh=fine,
        in_specs=placed,
        out_specs=(P("b", GRID), P("b", None)),
        check_vma=False,
    )
```

time: 791 us -> 304 us (0.38)
  waiting for transfers between devices: 366 us -> 88.4 us
  other arithmetic: 273 us -> 0.52 us
  starting transfers between devices: 5.74 us -> 94.5 us
  Pallas kernels: 0 us -> 77.3 us
  matrix products: 75.5 us -> 17.4 us
  local copies, waits for them, and re-layouts: 41.8 us -> 5.88 us
    another operation x33 -> x1, other arithmetic: 256 us -> 0.08 us  [body(): jnp.stack([lax.axis_index(a) for a in ('b', 'c', 'x', 'z')])]
    psum x1, waiting for transfers between devices: 194 us -> 0.02 us  [body(): short = lax.psum(project(ids, near, far, stacked[:rows_q], panel), 'b')]
    all_gather x3 -> x0, waiting for transfers between devices: 100 us -> none  [the longest x1 53.2 us: body(): both = tdot(stacked, lax.all_gather(panel, 'band', axis=0, tiled=True))]
    ppermute x0 -> x46, starting transfers between devices: none -> 94.4 us  [shift(): lax.ppermute(array, axis, [(i, (i + by) % count) for i in range(count)])]
    ppermute x0 -> x46, waiting for transfers between devices: none -> 88.4 us  [shift(): lax.ppermute(array, axis, [(i, (i + by) % count) for i in range(count)])]
    pallas_call x0 -> x5, Pallas kernels: none -> 77.3 us  [the longest x1 58.2 us: factor_rows(): pl.pallas_call(factor_body, out_shape=jax.ShapeDtypeStruct((n // B, n), F...]
    all_to_all x1 -> x0, waiting for transfers between devices: 70.9 us -> none  [summed_on_arrival(): lax.all_to_all(blocks, axis, split_axis=0, concat_axis=0, tiled=True)]
    another operation x29 -> x0, matrix products: 36.1 us -> none  [the longest x14 23.1 us: body(): factor = jnp.linalg.cholesky(gram)]
  transfers between devices with their start and end apart: 6 -> 47, of which waited for: 4 -> 23; matrix products, arithmetic and copies ran while one was open for 45% -> 3% of each run, Pallas kernels for 0% -> 24%
where the time goes in v1:
time: 304 us; the launch traced here: 299 us
  starting transfers between devices  94.5 us (31%)
  waiting for transfers between devices  88.4 us (29%)
  Pallas kernels  77.3 us (25%)
  matrix products  17.4 us (6%)
  between operations  14.8 us (5%)
  local copies, waits for them, and re-layouts  5.88 us (2%)
    ppermute x46, starting transfers between devices, shift(): lax.ppermute(array, axis, [(i, (i + by) % count) for i in range(count)])  94.4 us
    ppermute x46, waiting for transfers between devices, shift(): lax.ppermute(array, axis, [(i, (i + by) % count) for i in range(count)])  88.4 us
    pallas_call x1, Pallas kernels, factor_rows(): pl.pallas_call(factor_body, out_shape=jax.ShapeDtypeStruct((n // B, n), F...  58.2 us
    dot_general x4, matrix products, tdot(): lax.dot_general(left, right, (((1,), (1,)), ((), ())), precision=HI, pref...  10.6 us
    pallas_call x1, Pallas kernels, project(): pl.pallas_call(project_body, out_shape=jax.ShapeDtypeStruct((cols, pts),...  8.58 us
    dot_general x1, matrix products, body(): new_panel = jnp.dot(rows, short, precision=HI, preferred_element_type=F32)  6.83 us
  transfers between devices with their start and end apart: 47, of which 23 were waited for; matrix products, arithmetic and copies ran while one was open for 3% of the time, Pallas kernels for 24%

profile of v1, /device:TPU:57, one launch (start us, length us, event | category | flops | bytes accessed | tf_op | source)
XLA Modules:
  0.0 298.8 jit_solution(454273132726443788)
XLA Ops:
  7.7 2.2 collective-permute-start.2
  12.9 2.4 rotate.1
  15.3 2.6 fusion.6
  18.0 14.7 %collective-permute-done = f32[256,1024]{1,0:T(8,128)S(1)} collective-permute-done((f32[256,1024]{1,0:T(8,128)}, f32[256,1024]{1,0:T(8,128)S(1)}, u32[]{:S(2)}, u32[]{:S(2)}) %collective-permute-start) | collective-permute-done | bytes 1048608 | tf_op jit(solution)/shard_map/ppermute | solution.py:22
  32.9 2.9 collective-permute-start.3
  35.8 2.6 fusion.4
  38.6 2.7 fusion
  41.2 4.8 %collective-permute-done.1 = f32[128,1024]{1,0:T(8,128)S(1)} collective-permute-done((f32[128,1024]{1,0:T(8,128)S(1)}, f32[128,1024]{1,0:T(8,128)S(1)}, u32[]{:S(2)}, u32[]{:S(2)}) %collective-permute-start.1) | collective-permute-done | bytes 524320 | tf_op jit(solution)/shard_map/ppermute | solution.py:22
  46.0 2.7 fusion.2
  49.0 2.5 collective-permute-start.4
  51.5 3.0 %collective-permute-done.4 = f32[256,1536]{1,0:T(8,128)S(1)} collective-permute-done((f32[256,1536]{1,0:T(8,128)S(1)}, f32[256,1536]{1,0:T(8,128)S(1)}, u32[]{:S(2)}, u32[]{:S(2)}) %collective-permute-start.4) | collective-permute-done | bytes 1572896 | tf_op jit(solution)/shard_map/ppermute | solution.py:22
  60.6 10.9 %collective-permute-done.7 = f32[32,1536]{1,0:T(8,128)S(1)} collective-permute-done((f32[32,1536]{1,0:T(8,128)S(1)}, f32[32,1536]{1,0:T(8,128)S(1)}, u32[]{:S(2)}, u32[]{:S(2)}) %collective-permute-start.7) | collective-permute-done | bytes 196640 | tf_op jit(solution)/shard_map/ppermute | solution.py:22
  71.5 4.2 %collective-permute-done.8 = f32[32,1536]{1,0:T(8,128)S(1)} collective-permute-done((f32[32,1536]{1,0:T(8,128)S(1)}, f32[32,1536]{1,0:T(8,128)S(1)}, u32[]{:S(2)}, u32[]{:S(2)}) %collective-permute-start.8) | collective-permute-done | bytes 196640 | tf_op jit(solution)/shard_map/ppermute | solution.py:22
  75.9 2.1 collective-permute-start.9
  78.0 4.9 %collective-permute-start.14 = (f32[8,1536]{1,0:T(8,128)S(1)}, f32[8,1536]{1,0:T(8,128)S(1)}, u32[]{:S(2)}, u32[]{:S(2)}) collective-permute-start(f32[8,1536]{1,0:T(8,128)S(1)} %get-tuple-element.22), channel_id=1, source_target_pairs={{0,192},{32,224},{64,0},{96,32},{128,64},{160,96},{192,128},{224,1... | collective-permute-start | bytes 147464 | tf_op jit(solution)/shard_map/ppermute | solution.py:22
  83.0 2.8 collective-permute-start.13
  87.2 2.7 collective-permute-start.11
  90.7 3.0 %collective-permute-done.12 = f32[8,1536]{1,0:T(8,128)S(1)} collective-permute-done((f32[8,1536]{1,0:T(8,128)S(1)}, f32[8,1536]{1,0:T(8,128)S(1)}, u32[]{:S(2)}, u32[]{:S(2)}) %collective-permute-start.12) | collective-permute-done | bytes 49184 | tf_op jit(solution)/shard_map/ppermute | solution.py:22
  95.7 2.1 collective-permute-done.10
  101.1 3.7 %collective-permute-start.19 = (f32[8,1024]{1,0:T(8,128)S(1)}, f32[8,1024]{1,0:T(8,128)S(1)}, u32[]{:S(2)}, u32[]{:S(2)}) collective-permute-start(f32[8,1024]{1,0:T(8,128)S(1)} %get-tuple-element.46), channel_id=1, source_target_pairs={{0,128},{32,160},{64,192},{96,224},{128,0},{160,32},{192,64},{224,... | collective-permute-start | bytes 98312 | tf_op jit(solution)/shard_map/ppermute | solution.py:22
  104.8 3.0 %collective-permute-start.17 = (f32[8,1024]{1,0:T(8,128)S(1)}, f32[8,1024]{1,0:T(8,128)S(1)}, u32[]{:S(2)}, u32[]{:S(2)}) collective-permute-start(f32[8,1024]{1,0:T(8,128)S(1)} %get-tuple-element.46), channel_id=1, source_target_pairs={{0,192},{32,224},{64,0},{96,32},{128,64},{160,96},{192,128},{224,1... | collective-permute-start | bytes 98312 | tf_op jit(solution)/shard_map/ppermute | solution.py:22
  108.9 3.7 %collective-permute-start.18 = (f32[8,1024]{1,0:T(8,128)S(1)}, f32[8,1024]{1,0:T(8,128)S(1)}, u32[]{:S(2)}, u32[]{:S(2)}) collective-permute-start(f32[8,1024]{1,0:T(8,128)S(1)} %get-tuple-element.46), channel_id=1, source_target_pairs={{0,160},{32,192},{64,224},{96,0},{128,32},{160,64},{192,96},{224,1... | collective-permute-start | bytes 98312 | tf_op jit(solution)/shard_map/ppermute | solution.py:22
  112.5 2.2 collective-permute-done.18
  114.8 2.6 collective-permute-start.23
  117.4 3.3 %collective-permute-done.23 = f32[64,1024]{1,0:T(8,128)S(1)} collective-permute-done((f32[64,1024]{1,0:T(8,128)S(1)}, f32[64,1024]{1,0:T(8,128)S(1)}, u32[]{:S(2)}, u32[]{:S(2)}) %collective-permute-start.23) | collective-permute-done | bytes 262176 | tf_op jit(solution)/shard_map/ppermute | solution.py:22
  120.7 3.4 %collective-permute-start.24 = (f32[32,1024]{1,0:T(8,128)S(1)}, f32[32,1024]{1,0:T(8,128)S(1)}, u32[]{:S(2)}, u32[]{:S(2)}) collective-permute-start(f32[32,1024]{1,0:T(8,128)S(1)} %slice.196), channel_id=1, source_target_pairs={{0,24},{8,0},{16,8},{24,16},{1,25},{9,1},{17,9},{25,17},{2,26},{10... | collective-permute-start | bytes 393224 | tf_op jit(solution)/shard_map/ppermute | solution.py:22
  124.2 3.2 %collective-permute-done.24 = f32[32,1024]{1,0:T(8,128)S(1)} collective-permute-done((f32[32,1024]{1,0:T(8,128)S(1)}, f32[32,1024]{1,0:T(8,128)S(1)}, u32[]{:S(2)}, u32[]{:S(2)}) %collective-permute-start.24) | collective-permute-done | bytes 131104 | tf_op jit(solution)/shard_map/ppermute | solution.py:22
  127.4 3.5 %collective-permute-done.26 = f32[32,1024]{1,0:T(8,128)S(1)} collective-permute-done((f32[32,1024]{1,0:T(8,128)S(1)}, f32[32,1024]{1,0:T(8,128)S(1)}, u32[]{:S(2)}, u32[]{:S(2)}) %collective-permute-start.26) | collective-permute-done | bytes 131104 | tf_op jit(solution)/shard_map/ppermute | solution.py:22
  130.9 7.3 %collective-permute-start.27 = (f32[256,1024]{1,0:T(8,128)S(1)}, f32[256,1024]{1,0:T(8,128)S(1)}, u32[]{:S(2)}, u32[]{:S(2)}) collective-permute-start(f32[256,1024]{1,0:T(8,128)S(1)} %constant_dynamic-update-slice_fusion.8.near_ref), channel_id=1, source_target_pairs={{0,4},{4,0},{1,5},{5,1},{2,6},{6,2},{3,7},{7,3},{8,12},{12,8},{9,1... | collective-permute-start | bytes 3145736 | tf_op jit(solution)/shard_map/ppermute | solution.py:22
  138.3 2.3 collective-permute-done.27.far_ref
  140.6 4.7 %squares.1 = f32[4,8,512]{2,1,0:T(8,128)S(1)} custom-call(s32[4]{0:T(128)S(1)} %pad_add_fusion.ids_ref, f32[256,1024]{1,0:T(8,128)S(1)} %constant_dynamic-update-slice_fusion.8.near_ref, f32[256,1024]{1,0:T(8,128)S(1)} %collective-permute-done.27.far_ref), custom_call_target="tpu_custom_call" | custom-call | tf_op jit(solution)/shard_map/squares/pallas_call | solution.py:114
  145.3 3.1 %collective-permute-start.28 = (f32[8,512]{1,0:T(8,128)S(1)}, f32[8,512]{1,0:T(8,128)S(1)}, u32[]{:S(2)}, u32[]{:S(2)}) collective-permute-start(f32[8,512]{1,0:T(8,128)S(1)} %get-tuple-element.41), channel_id=1, source_target_pairs={{0,1},{1,2},{2,3},{3,0},{4,5},{5,6},{6,7},{7,4},{8,9},{9,10},{10,1... | collective-permute-start | bytes 49160 | tf_op jit(solution)/shard_map/ppermute | solution.py:22
  149.8 8.6 %project.1 = f32[1024,1024]{1,0:T(8,128)S(1)} custom-call(s32[4]{0:T(128)S(1)} %pad_add_fusion.ids_ref, f32[256,1024]{1,0:T(8,128)S(1)} %constant_dynamic-update-slice_fusion.8.near_ref, f32[256,1024]{1,0:T(8,128)S(1)} %collective-permute-done.27.far_ref, f32[512,1024]{1,0:T(8,128)S(1)} %slice_bitcast_fusion.basis_ref, f32[256,1024]{1,0:T(8,128)S(1)} %copy-done.2), custom_call_target="tpu_custom_call" | custom-call | tf_op jit(solution)/shard_map/project/pallas_call | solution.py:137
  162.0 2.4 collective-permute-start.32
  166.1 2.1 collective-permute-done.31
  171.0 3.1 %collective-permute-start.38 = (f32[32,512]{1,0:T(8,128)S(1)}, f32[32,512]{1,0:T(8,128)S(1)}, u32[]{:S(2)}, u32[]{:S(2)}) collective-permute-start(f32[32,512]{1,0:T(8,128)S(1)} %pad_maximum_fusion), channel_id=1, source_target_pairs={{0,96},{32,128},{64,160},{96,192},{128,224},{160,0},{192,32},{224,... | collective-permute-start | bytes 196616 | tf_op jit(solution)/shard_map/ppermute | solution.py:22
  174.1 2.5 collective-permute-start.37
  176.7 3.4 %collective-permute-done.34 = f32[32,512]{1,0:T(8,128)S(1)} collective-permute-done((f32[32,512]{1,0:T(8,128)S(1)}, f32[32,512]{1,0:T(8,128)S(1)}, u32[]{:S(2)}, u32[]{:S(2)}) %collective-permute-start.34) | collective-permute-done | bytes 65568 | tf_op jit(solution)/shard_map/ppermute | solution.py:22
  180.1 3.2 %collective-permute-start.35 = (f32[32,512]{1,0:T(8,128)S(1)}, f32[32,512]{1,0:T(8,128)S(1)}, u32[]{:S(2)}, u32[]{:S(2)}) collective-permute-start(f32[32,512]{1,0:T(8,128)S(1)} %pad_maximum_fusion), channel_id=1, source_target_pairs={{0,192},{32,224},{64,0},{96,32},{128,64},{160,96},{192,128},{224,1... | collective-permute-start | bytes 196616 | tf_op jit(solution)/shard_map/ppermute | solution.py:22
  184.9 4.0 %collective-permute-start.36 = (f32[32,512]{1,0:T(8,128)S(1)}, f32[32,512]{1,0:T(8,128)S(1)}, u32[]{:S(2)}, u32[]{:S(2)}) collective-permute-start(f32[32,512]{1,0:T(8,128)S(1)} %pad_maximum_fusion), channel_id=1, source_target_pairs={{0,160},{32,192},{64,224},{96,0},{128,32},{160,64},{192,96},{224,1... | collective-permute-start | bytes 196616 | tf_op jit(solution)/shard_map/ppermute | solution.py:22
  188.9 2.8 collective-permute-done.36
  193.5 7.0 %collective-permute-done.41 = f32[256,512]{1,0:T(8,128)S(1)} collective-permute-done((f32[256,512]{1,0:T(8,128)S(1)}, f32[256,512]{1,0:T(8,128)S(1)}, u32[]{:S(2)}, u32[]{:S(2)}) %collective-permute-start.41) | collective-permute-done | bytes 524320 | tf_op jit(solution)/shard_map/ppermute | solution.py:22
  202.1 5.7 %collective-permute-done.42 = f32[128,512]{1,0:T(8,128)S(1)} collective-permute-done((f32[128,512]{1,0:T(8,128)S(1)}, f32[128,512]{1,0:T(8,128)S(1)}, u32[]{:S(2)}, u32[]{:S(2)}) %collective-permute-start.42) | collective-permute-done | bytes 262176 | tf_op jit(solution)/shard_map/ppermute | solution.py:22
  207.9 3.3 %collective-permute-done.44 = f32[128,512]{1,0:T(8,128)S(1)} collective-permute-done((f32[128,512]{1,0:T(8,128)S(1)}, f32[128,512]{1,0:T(8,128)S(1)}, u32[]{:S(2)}, u32[]{:S(2)}) %collective-permute-start.44) | collective-permute-done | bytes 262176 | tf_op jit(solution)/shard_map/ppermute | solution.py:22
  211.3 11.6 %collective-permute-start.45 = (f32[1024,512]{1,0:T(8,128)S(1)}, f32[1024,512]{1,0:T(8,128)S(1)}, u32[]{:S(2)}, u32[]{:S(2)}) collective-permute-start(f32[1024,512]{1,0:T(8,128)S(1)} %constant_dynamic-update-slice_fusion.31), channel_id=1, source_target_pairs={{0,4},{4,0},{1,5},{5,1},{2,6},{6,2},{3,7},{7,3},{8,12},{12,8},{9,1... | collective-permute-start | bytes 6291464 | tf_op jit(solution)/shard_map/ppermute | solution.py:22
  222.9 3.4 %unrotate.1 = f32[64,8,1024]{2,1,0:T(8,128)} custom-call(s32[4]{0:T(128)S(1)} %pad_add_fusion.ids_ref, f32[32,8,1024]{2,1,0:T(8,128)S(1)} %bitcast.49, f32[32,8,1024]{2,1,0:T(8,128)S(1)} %bitcast.51), custom_call_target="tpu_custom_call" | custom-call | tf_op jit(solution)/shard_map/unrotate/pallas_call | solution.py:84
  226.6 58.2 %factor_rows.1 = f32[256,1024]{1,0:T(8,128)S(1)} custom-call(s32[4]{0:T(128)S(1)} %pad_add_fusion.ids_ref, f32[128,8,512]{2,1,0:T(8,128)S(1)} %bitcast.52, f32[128,8,512]{2,1,0:T(8,128)S(1)} %bitcast.54), custom_call_target="tpu_custom_call" | custom-call | tf_op jit(solution)/shard_map/factor_rows/pallas_call | solution.py:257
  284.8 6.8 %fusion.28 = f32[256,1024]{1,0:T(8,128)} fusion(f32[256,1024]{1,0:T(8,128)S(1)} %factor_rows.1, f32[1024,1024]{1,0:T(8,128)} %all-reduce.2.cloned.1.call-done), kind=kOutput, calls=%fused_computation.96 | convolution fusion | flops 3221225472 | bytes 6291456 | tf_op jit(solution)/shard_map/dot_general | solution.py:331
  (115 shorter events, 34.0 us)
Async XLA Ops:
  7.2 277.7 %all-reduce.2.cloned.1.call-start = ((), (), s32[]{:S(2)}) async-start(), calls=%async_computation | async-start | bytes 8388608 | tf_op jit(solution)/shard_map/psum | solution.py:327
  7.2 25.5 %collective-permute-start = (f32[256,1024]{1,0:T(8,128)}, f32[256,1024]{1,0:T(8,128)S(1)}, u32[]{:S(2)}, u32[]{:S(2)}) collective-permute-start(f32[256,1024]{1,0:T(8,128)} %panel_ref.1), channel_id=1, source_target_pairs={{0,3},{1,0},{2,1},{3,2},{4,7},{5,4},{6,5},{7,6},{8,11},{9,8},{10,9... | collective-permute-start | bytes 3145736 | tf_op jit(solution)/shard_map/ppermute | solution.py:22
  7.7 25.1 %collective-permute-start.2 = (f32[256,1024]{1,0:T(8,128)}, f32[256,1024]{1,0:T(8,128)S(1)}, u32[]{:S(2)}, u32[]{:S(2)}) collective-permute-start(f32[256,1024]{1,0:T(8,128)} %panel_ref.1), channel_id=1, source_target_pairs={{0,1},{1,2},{2,3},{3,0},{4,5},{5,6},{6,7},{7,4},{8,9},{9,10},{10,1... | collective-permute-start | bytes 3145736 | tf_op jit(solution)/shard_map/ppermute | solution.py:22
  12.9 2.4 copy-start.2
  32.8 13.2 %collective-permute-start.1 = (f32[128,1024]{1,0:T(8,128)S(1)}, f32[128,1024]{1,0:T(8,128)S(1)}, u32[]{:S(2)}, u32[]{:S(2)}) collective-permute-start(f32[128,1024]{1,0:T(8,128)S(1)} %slice.169), channel_id=1, source_target_pairs={{0,3},{1,0},{2,1},{3,2},{4,7},{5,4},{6,5},{7,6},{8,11},{9,8},{10,9... | collective-permute-start | bytes 1572872 | tf_op jit(solution)/shard_map/ppermute | solution.py:22
  32.9 13.1 %collective-permute-start.3 = (f32[128,1024]{1,0:T(8,128)S(1)}, f32[128,1024]{1,0:T(8,128)S(1)}, u32[]{:S(2)}, u32[]{:S(2)}) collective-permute-start(f32[128,1024]{1,0:T(8,128)S(1)} %slice.170), channel_id=1, source_target_pairs={{0,1},{1,2},{2,3},{3,0},{4,5},{5,6},{6,7},{7,4},{8,9},{9,10},{10,1... | collective-permute-start | bytes 1572872 | tf_op jit(solution)/shard_map/ppermute | solution.py:22
  49.0 5.5 %collective-permute-start.4 = (f32[256,1536]{1,0:T(8,128)S(1)}, f32[256,1536]{1,0:T(8,128)S(1)}, u32[]{:S(2)}, u32[]{:S(2)}) collective-permute-start(f32[256,1536]{1,0:T(8,128)S(1)} %get-tuple-element.8), channel_id=1, source_target_pairs={{0,4},{4,0},{1,5},{5,1},{2,6},{6,2},{3,7},{7,3},{8,12},{12,8},{9,1... | collective-permute-start | bytes 4718600 | tf_op jit(solution)/shard_map/ppermute | solution.py:22
  54.8 21.0 %collective-permute-start.5 = (f32[64,1536]{1,0:T(8,128)S(1)}, f32[64,1536]{1,0:T(8,128)S(1)}, u32[]{:S(2)}, u32[]{:S(2)}) collective-permute-start(f32[64,1536]{1,0:T(8,128)S(1)} %get-tuple-element.6), channel_id=1, source_target_pairs={{0,8},{8,16},{16,24},{24,0},{1,9},{9,17},{17,25},{25,1},{2,10},{10... | collective-permute-start | bytes 1179656 | tf_op jit(solution)/shard_map/ppermute | solution.py:22
  56.0 19.7 %collective-permute-start.6 = (f32[64,1536]{1,0:T(8,128)S(1)}, f32[64,1536]{1,0:T(8,128)S(1)}, u32[]{:S(2)}, u32[]{:S(2)}) collective-permute-start(f32[64,1536]{1,0:T(8,128)S(1)} %get-tuple-element.7), channel_id=1, source_target_pairs={{0,24},{8,0},{16,8},{24,16},{1,25},{9,1},{17,9},{25,17},{2,26},{10... | collective-permute-start | bytes 1179656 | tf_op jit(solution)/shard_map/ppermute | solution.py:22
  57.5 14.0 %collective-permute-start.7 = (f32[32,1536]{1,0:T(8,128)S(1)}, f32[32,1536]{1,0:T(8,128)S(1)}, u32[]{:S(2)}, u32[]{:S(2)}) collective-permute-start(f32[32,1536]{1,0:T(8,128)S(1)} %get-tuple-element.4), channel_id=1, source_target_pairs={{0,16},{8,24},{16,0},{24,8},{1,17},{9,25},{17,1},{25,9},{2,18},{10... | collective-permute-start | bytes 589832 | tf_op jit(solution)/shard_map/ppermute | solution.py:22
  59.2 16.6 %collective-permute-start.8 = (f32[32,1536]{1,0:T(8,128)S(1)}, f32[32,1536]{1,0:T(8,128)S(1)}, u32[]{:S(2)}, u32[]{:S(2)}) collective-permute-start(f32[32,1536]{1,0:T(8,128)S(1)} %get-tuple-element.5), channel_id=1, source_target_pairs={{0,16},{8,24},{16,0},{24,8},{1,17},{9,25},{17,1},{25,9},{2,18},{10... | collective-permute-start | bytes 589832 | tf_op jit(solution)/shard_map/ppermute | solution.py:22
  75.9 11.4 %collective-permute-start.9 = (f32[8,1536]{1,0:T(8,128)S(1)}, f32[8,1536]{1,0:T(8,128)S(1)}, u32[]{:S(2)}, u32[]{:S(2)}) collective-permute-start(f32[8,1536]{1,0:T(8,128)S(1)} %get-tuple-element.20), channel_id=1, source_target_pairs={{0,32},{32,64},{64,96},{96,128},{128,160},{160,192},{192,224},{224... | collective-permute-start | bytes 147464 | tf_op jit(solution)/shard_map/ppermute | solution.py:22
  78.0 12.0 %collective-permute-start.15 = (f32[8,1536]{1,0:T(8,128)S(1)}, f32[8,1536]{1,0:T(8,128)S(1)}, u32[]{:S(2)}, u32[]{:S(2)}) collective-permute-start(f32[8,1536]{1,0:T(8,128)S(1)} %get-tuple-element.21), channel_id=1, source_target_pairs={{0,224},{32,0},{64,32},{96,64},{128,96},{160,128},{192,160},{224,1... | collective-permute-start | bytes 147464 | tf_op jit(solution)/shard_map/ppermute | solution.py:22
  78.0 12.7 %collective-permute-start.14 = (f32[8,1536]{1,0:T(8,128)S(1)}, f32[8,1536]{1,0:T(8,128)S(1)}, u32[]{:S(2)}, u32[]{:S(2)}) collective-permute-start(f32[8,1536]{1,0:T(8,128)S(1)} %get-tuple-element.22), channel_id=1, source_target_pairs={{0,192},{32,224},{64,0},{96,32},{128,64},{160,96},{192,128},{224,1... | collective-permute-start | bytes 147464 | tf_op jit(solution)/shard_map/ppermute | solution.py:22
  83.0 7.7 %collective-permute-start.13 = (f32[8,1536]{1,0:T(8,128)S(1)}, f32[8,1536]{1,0:T(8,128)S(1)}, u32[]{:S(2)}, u32[]{:S(2)}) collective-permute-start(f32[8,1536]{1,0:T(8,128)S(1)} %get-tuple-element.23), channel_id=1, source_target_pairs={{0,160},{32,192},{64,224},{96,0},{128,32},{160,64},{192,96},{224,1... | collective-permute-start | bytes 147464 | tf_op jit(solution)/shard_map/ppermute | solution.py:22
  85.8 7.9 %collective-permute-start.12 = (f32[8,1536]{1,0:T(8,128)S(1)}, f32[8,1536]{1,0:T(8,128)S(1)}, u32[]{:S(2)}, u32[]{:S(2)}) collective-permute-start(f32[8,1536]{1,0:T(8,128)S(1)} %get-tuple-element.24), channel_id=1, source_target_pairs={{0,128},{32,160},{64,192},{96,224},{128,0},{160,32},{192,64},{224,... | collective-permute-start | bytes 147464 | tf_op jit(solution)/shard_map/ppermute | solution.py:22
  87.2 8.5 %collective-permute-start.11 = (f32[8,1536]{1,0:T(8,128)S(1)}, f32[8,1536]{1,0:T(8,128)S(1)}, u32[]{:S(2)}, u32[]{:S(2)}) collective-permute-start(f32[8,1536]{1,0:T(8,128)S(1)} %get-tuple-element.25), channel_id=1, source_target_pairs={{0,96},{32,128},{64,160},{96,192},{128,224},{160,0},{192,32},{224,... | collective-permute-start | bytes 147464 | tf_op jit(solution)/shard_map/ppermute | solution.py:22
  90.0 7.9 %collective-permute-start.10 = (f32[8,1536]{1,0:T(8,128)S(1)}, f32[8,1536]{1,0:T(8,128)S(1)}, u32[]{:S(2)}, u32[]{:S(2)}) collective-permute-start(f32[8,1536]{1,0:T(8,128)S(1)} %get-tuple-element.26), channel_id=1, source_target_pairs={{0,64},{32,96},{64,128},{96,160},{128,192},{160,224},{192,0},{224,... | collective-permute-start | bytes 147464 | tf_op jit(solution)/shard_map/ppermute | solution.py:22
  97.9 6.9 %collective-permute-start.16 = (f32[8,1024]{1,0:T(8,128)S(1)}, f32[8,1024]{1,0:T(8,128)S(1)}, u32[]{:S(2)}, u32[]{:S(2)}) collective-permute-start(f32[8,1024]{1,0:T(8,128)S(1)} %get-tuple-element.46), channel_id=1, source_target_pairs={{0,224},{32,0},{64,32},{96,64},{128,96},{160,128},{192,160},{224,1... | collective-permute-start | bytes 98312 | tf_op jit(solution)/shard_map/ppermute | solution.py:22
  98.6 16.2 %collective-permute-start.22 = (f32[8,1024]{1,0:T(8,128)S(1)}, f32[8,1024]{1,0:T(8,128)S(1)}, u32[]{:S(2)}, u32[]{:S(2)}) collective-permute-start(f32[8,1024]{1,0:T(8,128)S(1)} %get-tuple-element.46), channel_id=1, source_target_pairs={{0,32},{32,64},{64,96},{96,128},{128,160},{160,192},{192,224},{224... | collective-permute-start | bytes 98312 | tf_op jit(solution)/shard_map/ppermute | solution.py:22
  99.4 15.3 %collective-permute-start.21 = (f32[8,1024]{1,0:T(8,128)S(1)}, f32[8,1024]{1,0:T(8,128)S(1)}, u32[]{:S(2)}, u32[]{:S(2)}) collective-permute-start(f32[8,1024]{1,0:T(8,128)S(1)} %get-tuple-element.46), channel_id=1, source_target_pairs={{0,64},{32,96},{64,128},{96,160},{128,192},{160,224},{192,0},{224,... | collective-permute-start | bytes 98312 | tf_op jit(solution)/shard_map/ppermute | solution.py:22
  100.0 14.8 %collective-permute-start.20 = (f32[8,1024]{1,0:T(8,128)S(1)}, f32[8,1024]{1,0:T(8,128)S(1)}, u32[]{:S(2)}, u32[]{:S(2)}) collective-permute-start(f32[8,1024]{1,0:T(8,128)S(1)} %get-tuple-element.46), channel_id=1, source_target_pairs={{0,96},{32,128},{64,160},{96,192},{128,224},{160,0},{192,32},{224,... | collective-permute-start | bytes 98312 | tf_op jit(solution)/shard_map/ppermute | solution.py:22
  101.1 13.6 %collective-permute-start.19 = (f32[8,1024]{1,0:T(8,128)S(1)}, f32[8,1024]{1,0:T(8,128)S(1)}, u32[]{:S(2)}, u32[]{:S(2)}) collective-permute-start(f32[8,1024]{1,0:T(8,128)S(1)} %get-tuple-element.46), channel_id=1, source_target_pairs={{0,128},{32,160},{64,192},{96,224},{128,0},{160,32},{192,64},{224,... | collective-permute-start | bytes 98312 | tf_op jit(solution)/shard_map/ppermute | solution.py:22
  104.8 4.0 %collective-permute-start.17 = (f32[8,1024]{1,0:T(8,128)S(1)}, f32[8,1024]{1,0:T(8,128)S(1)}, u32[]{:S(2)}, u32[]{:S(2)}) collective-permute-start(f32[8,1024]{1,0:T(8,128)S(1)} %get-tuple-element.46), channel_id=1, source_target_pairs={{0,192},{32,224},{64,0},{96,32},{128,64},{160,96},{192,128},{224,1... | collective-permute-start | bytes 98312 | tf_op jit(solution)/shard_map/ppermute | solution.py:22
  108.9 5.9 %collective-permute-start.18 = (f32[8,1024]{1,0:T(8,128)S(1)}, f32[8,1024]{1,0:T(8,128)S(1)}, u32[]{:S(2)}, u32[]{:S(2)}) collective-permute-start(f32[8,1024]{1,0:T(8,128)S(1)} %get-tuple-element.46), channel_id=1, source_target_pairs={{0,160},{32,192},{64,224},{96,0},{128,32},{160,64},{192,96},{224,1... | collective-permute-start | bytes 98312 | tf_op jit(solution)/shard_map/ppermute | solution.py:22
  114.8 5.9 %collective-permute-start.23 = (f32[64,1024]{1,0:T(8,128)S(1)}, f32[64,1024]{1,0:T(8,128)S(1)}, u32[]{:S(2)}, u32[]{:S(2)}) collective-permute-start(f32[64,1024]{1,0:T(8,128)S(1)} %get-tuple-element.47), channel_id=1, source_target_pairs={{0,24},{8,0},{16,8},{24,16},{1,25},{9,1},{17,9},{25,17},{2,26},{10... | collective-permute-start | bytes 786440 | tf_op jit(solution)/shard_map/ppermute | solution.py:22
  117.4 6.7 %collective-permute-start.25 = (f32[64,1024]{1,0:T(8,128)S(1)}, f32[64,1024]{1,0:T(8,128)S(1)}, u32[]{:S(2)}, u32[]{:S(2)}) collective-permute-start(f32[64,1024]{1,0:T(8,128)S(1)} %get-tuple-element.47), channel_id=1, source_target_pairs={{0,8},{8,16},{16,24},{24,0},{1,9},{9,17},{17,25},{25,1},{2,10},{10... | collective-permute-start | bytes 786440 | tf_op jit(solution)/shard_map/ppermute | solution.py:22
  120.7 6.7 %collective-permute-start.24 = (f32[32,1024]{1,0:T(8,128)S(1)}, f32[32,1024]{1,0:T(8,128)S(1)}, u32[]{:S(2)}, u32[]{:S(2)}) collective-permute-start(f32[32,1024]{1,0:T(8,128)S(1)} %slice.196), channel_id=1, source_target_pairs={{0,24},{8,0},{16,8},{24,16},{1,25},{9,1},{17,9},{25,17},{2,26},{10... | collective-permute-start | bytes 393224 | tf_op jit(solution)/shard_map/ppermute | solution.py:22
  124.1 6.8 %collective-permute-start.26 = (f32[32,1024]{1,0:T(8,128)S(1)}, f32[32,1024]{1,0:T(8,128)S(1)}, u32[]{:S(2)}, u32[]{:S(2)}) collective-permute-start(f32[32,1024]{1,0:T(8,128)S(1)} %slice.197), channel_id=1, source_target_pairs={{0,8},{8,16},{16,24},{24,0},{1,9},{9,17},{17,25},{25,1},{2,10},{10... | collective-permute-start | bytes 393224 | tf_op jit(solution)/shard_map/ppermute | solution.py:22
  130.9 9.6 %collective-permute-start.27 = (f32[256,1024]{1,0:T(8,128)S(1)}, f32[256,1024]{1,0:T(8,128)S(1)}, u32[]{:S(2)}, u32[]{:S(2)}) collective-permute-start(f32[256,1024]{1,0:T(8,128)S(1)} %constant_dynamic-update-slice_fusion.8.near_ref), channel_id=1, source_target_pairs={{0,4},{4,0},{1,5},{5,1},{2,6},{6,2},{3,7},{7,3},{8,12},{12,8},{9,1... | collective-permute-start | bytes 3145736 | tf_op jit(solution)/shard_map/ppermute | solution.py:22
  145.3 15.2 %collective-permute-start.28 = (f32[8,512]{1,0:T(8,128)S(1)}, f32[8,512]{1,0:T(8,128)S(1)}, u32[]{:S(2)}, u32[]{:S(2)}) collective-permute-start(f32[8,512]{1,0:T(8,128)S(1)} %get-tuple-element.41), channel_id=1, source_target_pairs={{0,1},{1,2},{2,3},{3,0},{4,5},{5,6},{6,7},{7,4},{8,9},{9,10},{10,1... | collective-permute-start | bytes 49160 | tf_op jit(solution)/shard_map/ppermute | solution.py:22
  148.3 12.2 %collective-permute-start.30 = (f32[8,512]{1,0:T(8,128)S(1)}, f32[8,512]{1,0:T(8,128)S(1)}, u32[]{:S(2)}, u32[]{:S(2)}) collective-permute-start(f32[8,512]{1,0:T(8,128)S(1)} %get-tuple-element.42), channel_id=1, source_target_pairs={{0,3},{1,0},{2,1},{3,2},{4,7},{5,4},{6,5},{7,6},{8,11},{9,8},{10,9... | collective-permute-start | bytes 49160 | tf_op jit(solution)/shard_map/ppermute | solution.py:22
  148.3 12.2 %collective-permute-start.29 = (f32[8,512]{1,0:T(8,128)S(1)}, f32[8,512]{1,0:T(8,128)S(1)}, u32[]{:S(2)}, u32[]{:S(2)}) collective-permute-start(f32[8,512]{1,0:T(8,128)S(1)} %get-tuple-element.43), channel_id=1, source_target_pairs={{0,2},{1,3},{2,0},{3,1},{4,6},{5,7},{6,4},{7,5},{8,10},{9,11},{10,... | collective-permute-start | bytes 49160 | tf_op jit(solution)/shard_map/ppermute | solution.py:22
  160.5 3.9 %collective-permute-start.33 = (f32[8,512]{1,0:T(8,128)S(1)}, f32[8,512]{1,0:T(8,128)S(1)}, u32[]{:S(2)}, u32[]{:S(2)}) collective-permute-start(f32[8,512]{1,0:T(8,128)S(1)} %get-tuple-element.3), channel_id=1, source_target_pairs={{0,1},{1,2},{2,3},{3,0},{4,5},{5,6},{6,7},{7,4},{8,9},{9,10},{10,1... | collective-permute-start | bytes 49160 | tf_op jit(solution)/shard_map/ppermute | solution.py:22
  162.0 4.1 %collective-permute-start.32 = (f32[8,512]{1,0:T(8,128)S(1)}, f32[8,512]{1,0:T(8,128)S(1)}, u32[]{:S(2)}, u32[]{:S(2)}) collective-permute-start(f32[8,512]{1,0:T(8,128)S(1)} %get-tuple-element.3), channel_id=1, source_target_pairs={{0,2},{1,3},{2,0},{3,1},{4,6},{5,7},{6,4},{7,5},{8,10},{9,11},{10,... | collective-permute-start | bytes 49160 | tf_op jit(solution)/shard_map/ppermute | solution.py:22
  164.4 3.8 %collective-permute-start.31 = (f32[8,512]{1,0:T(8,128)S(1)}, f32[8,512]{1,0:T(8,128)S(1)}, u32[]{:S(2)}, u32[]{:S(2)}) collective-permute-start(f32[8,512]{1,0:T(8,128)S(1)} %get-tuple-element.3), channel_id=1, source_target_pairs={{0,3},{1,0},{2,1},{3,2},{4,7},{5,4},{6,5},{7,6},{8,11},{9,8},{10,9... | collective-permute-start | bytes 49160 | tf_op jit(solution)/shard_map/ppermute | solution.py:22
  168.2 23.7 %collective-permute-start.40 = (f32[32,512]{1,0:T(8,128)S(1)}, f32[32,512]{1,0:T(8,128)S(1)}, u32[]{:S(2)}, u32[]{:S(2)}) collective-permute-start(f32[32,512]{1,0:T(8,128)S(1)} %pad_maximum_fusion), channel_id=1, source_target_pairs={{0,32},{32,64},{64,96},{96,128},{128,160},{160,192},{192,224},{224... | collective-permute-start | bytes 196616 | tf_op jit(solution)/shard_map/ppermute | solution.py:22
  169.9 22.0 %collective-permute-start.39 = (f32[32,512]{1,0:T(8,128)S(1)}, f32[32,512]{1,0:T(8,128)S(1)}, u32[]{:S(2)}, u32[]{:S(2)}) collective-permute-start(f32[32,512]{1,0:T(8,128)S(1)} %pad_maximum_fusion), channel_id=1, source_target_pairs={{0,64},{32,96},{64,128},{96,160},{128,192},{160,224},{192,0},{224,... | collective-permute-start | bytes 196616 | tf_op jit(solution)/shard_map/ppermute | solution.py:22
  171.0 20.8 %collective-permute-start.38 = (f32[32,512]{1,0:T(8,128)S(1)}, f32[32,512]{1,0:T(8,128)S(1)}, u32[]{:S(2)}, u32[]{:S(2)}) collective-permute-start(f32[32,512]{1,0:T(8,128)S(1)} %pad_maximum_fusion), channel_id=1, source_target_pairs={{0,96},{32,128},{64,160},{96,192},{128,224},{160,0},{192,32},{224,... | collective-permute-start | bytes 196616 | tf_op jit(solution)/shard_map/ppermute | solution.py:22
  174.1 17.7 %collective-permute-start.37 = (f32[32,512]{1,0:T(8,128)S(1)}, f32[32,512]{1,0:T(8,128)S(1)}, u32[]{:S(2)}, u32[]{:S(2)}) collective-permute-start(f32[32,512]{1,0:T(8,128)S(1)} %pad_maximum_fusion), channel_id=1, source_target_pairs={{0,128},{32,160},{64,192},{96,224},{128,0},{160,32},{192,64},{224,... | collective-permute-start | bytes 196616 | tf_op jit(solution)/shard_map/ppermute | solution.py:22
  176.6 3.5 %collective-permute-start.34 = (f32[32,512]{1,0:T(8,128)S(1)}, f32[32,512]{1,0:T(8,128)S(1)}, u32[]{:S(2)}, u32[]{:S(2)}) collective-permute-start(f32[32,512]{1,0:T(8,128)S(1)} %pad_maximum_fusion), channel_id=1, source_target_pairs={{0,224},{32,0},{64,32},{96,64},{128,96},{160,128},{192,160},{224,1... | collective-permute-start | bytes 196616 | tf_op jit(solution)/shard_map/ppermute | solution.py:22
  180.1 4.8 %collective-permute-start.35 = (f32[32,512]{1,0:T(8,128)S(1)}, f32[32,512]{1,0:T(8,128)S(1)}, u32[]{:S(2)}, u32[]{:S(2)}) collective-permute-start(f32[32,512]{1,0:T(8,128)S(1)} %pad_maximum_fusion), channel_id=1, source_target_pairs={{0,192},{32,224},{64,0},{96,32},{128,64},{160,96},{192,128},{224,1... | collective-permute-start | bytes 196616 | tf_op jit(solution)/shard_map/ppermute | solution.py:22
  184.9 6.9 %collective-permute-start.36 = (f32[32,512]{1,0:T(8,128)S(1)}, f32[32,512]{1,0:T(8,128)S(1)}, u32[]{:S(2)}, u32[]{:S(2)}) collective-permute-start(f32[32,512]{1,0:T(8,128)S(1)} %pad_maximum_fusion), channel_id=1, source_target_pairs={{0,160},{32,192},{64,224},{96,0},{128,32},{160,64},{192,96},{224,1... | collective-permute-start | bytes 196616 | tf_op jit(solution)/shard_map/ppermute | solution.py:22
  191.9 8.5 %collective-permute-start.41 = (f32[256,512]{1,0:T(8,128)S(1)}, f32[256,512]{1,0:T(8,128)S(1)}, u32[]{:S(2)}, u32[]{:S(2)}) collective-permute-start(f32[256,512]{1,0:T(8,128)S(1)} %get-tuple-element.27), channel_id=1, source_target_pairs={{0,24},{8,0},{16,8},{24,16},{1,25},{9,1},{17,9},{25,17},{2,26},{10... | collective-permute-start | bytes 1572872 | tf_op jit(solution)/shard_map/ppermute | solution.py:22
  192.0 9.7 %collective-permute-start.43 = (f32[256,512]{1,0:T(8,128)S(1)}, f32[256,512]{1,0:T(8,128)S(1)}, u32[]{:S(2)}, u32[]{:S(2)}) collective-permute-start(f32[256,512]{1,0:T(8,128)S(1)} %get-tuple-element.27), channel_id=1, source_target_pairs={{0,8},{8,16},{16,24},{24,0},{1,9},{9,17},{17,25},{25,1},{2,10},{10... | collective-permute-start | bytes 1572872 | tf_op jit(solution)/shard_map/ppermute | solution.py:22
  200.5 7.4 %collective-permute-start.42 = (f32[128,512]{1,0:T(8,128)S(1)}, f32[128,512]{1,0:T(8,128)S(1)}, u32[]{:S(2)}, u32[]{:S(2)}) collective-permute-start(f32[128,512]{1,0:T(8,128)S(1)} %slice.202), channel_id=1, source_target_pairs={{0,24},{8,0},{16,8},{24,16},{1,25},{9,1},{17,9},{25,17},{2,26},{10... | collective-permute-start | bytes 786440 | tf_op jit(solution)/shard_map/ppermute | solution.py:22
  201.8 9.5 %collective-permute-start.44 = (f32[128,512]{1,0:T(8,128)S(1)}, f32[128,512]{1,0:T(8,128)S(1)}, u32[]{:S(2)}, u32[]{:S(2)}) collective-permute-start(f32[128,512]{1,0:T(8,128)S(1)} %slice.203), channel_id=1, source_target_pairs={{0,8},{8,16},{16,24},{24,0},{1,9},{9,17},{17,25},{25,1},{2,10},{10... | collective-permute-start | bytes 786440 | tf_op jit(solution)/shard_map/ppermute | solution.py:22
  211.3 15.3 %collective-permute-start.45 = (f32[1024,512]{1,0:T(8,128)S(1)}, f32[1024,512]{1,0:T(8,128)S(1)}, u32[]{:S(2)}, u32[]{:S(2)}) collective-permute-start(f32[1024,512]{1,0:T(8,128)S(1)} %constant_dynamic-update-slice_fusion.31), channel_id=1, source_target_pairs={{0,4},{4,0},{1,5},{5,1},{2,6},{6,2},{3,7},{7,3},{8,12},{12,8},{9,1... | collective-permute-start | bytes 6291464 | tf_op jit(solution)/shard_map/ppermute | solution.py:22
  (3 other events, 4.8 us)
Sparse Core Ops, SparseCore 0:
  160.6 94.9 all-reduce.1
